TPU v7x, 16 devices: a 4x2x1 block of a 4x4x8 slice. The times are simulated.
16 devices in a mesh: dp: 4 (over y, z, core), tp: 4 (over x).
Axes of the slice: x: 4, y: 2, z: 1, core: 2. Of those that a mesh axis runs over, the one named last changes fastest.
The devices are a block of a 4x4x8 slice.
Arguments:
- x: bfloat16 [2560, 7168], P(('dp', 'tp')), parts along dimension 0
- w_gate: bfloat16 [7168, 20480], P(None, 'tp')
- w_up: bfloat16 [7168, 20480], P(None, 'tp')
- w_down: bfloat16 [20480, 7168], P('tp')
Outputs:
- output: bfloat16 [2560, 7168], P(('dp', 'tp')), parts along dimension 0
There are 4 independent parts. A program takes and returns all parts, laid end to end along the dimension named above; an argument that names none is the same for every part.
All inputs are finite; a program needn't handle non-finite values.
Results may differ from a plain program's by a relative error of at most 0.016.
Values are sent between devices in bfloat16 or wider.
A program may use at most 768 MiB of HBM per device.

v0:
```python
import jax
import jax.numpy as jnp
from jax import lax
from jax.sharding import PartitionSpec as P


def solution(mesh):
    def step(x, w_gate, w_up, w_down):
        rows = lax.all_gather(x, "tp", axis=0, tiled=True)
        gate = jnp.dot(rows, w_gate, preferred_element_type=jnp.float32)
        up = jnp.dot(rows, w_up, preferred_element_type=jnp.float32)
        hidden = (jax.nn.silu(gate) * up).astype(jnp.bfloat16)
        term = jnp.dot(hidden, w_down, preferred_element_type=jnp.float32).astype(jnp.bfloat16)
        return lax.psum_scatter(term, "tp", scatter_dimension=0, tiled=True)

    return jax.shard_map(
        step,
        mesh=mesh,
        in_specs=(P(("dp", "tp"), None), P(None, "tp"), P(None, "tp"), P("tp", None)),
        out_specs=P(("dp", "tp"), None),
        check_vma=False,
    )
```

profile of v0, /device:TPU:112, one launch (start us, length us, event | category | flops | bytes accessed | tf_op | source)
XLA Modules:
  0.0 360.6 jit_solution(13752029759042371421)
XLA Ops:
  6.5 0.0 all-gather.2.cloned.1.call-start
  6.6 0.7 all-gather.2.cloned.1.call-update
  7.3 0.1 reduce-scatter.2.cloned.1.call-start
  7.4 90.4 %all-gather.2.cloned.1.call-done = bf16[640,7168]{1,0:T(8,128)(2,1)} async-done(((bf16[160,7168]{1,0:T(8,128)(2,1)}), bf16[640,7168]{1,0:T(8,128)(2,1)}) %all-gather.2.cloned.1.call-update) | async-done | bytes 9175056 | tf_op jit(solution)/shard_map/all_gather | solution.py:9
  97.7 57.5 %fusion = f32[640,5120]{1,0:T(8,128)} fusion(bf16[640,7168]{1,0:T(8,128)(2,1)} %all-gather.2.cloned.1.call-done, bf16[7168,5120]{1,0:T(8,128)(2,1)} %param.5), kind=kOutput, calls=%fused_computation.2 | convolution fusion | flops 46976204800 | bytes 95682560 | tf_op jit(solution)/shard_map/dot_general | solution.py:10
  155.2 59.0 %multiply_convert_fusion = bf16[640,5120]{1,0:T(8,128)(2,1)} fusion(f32[640,5120]{1,0:T(8,128)} %fusion, bf16[640,7168]{1,0:T(8,128)(2,1)} %all-gather.2.cloned.1.call-done, bf16[7168,5120]{1,0:T(8,128)(2,1)} %param.6), kind=kOutput, calls=%fused_computation | convolution fusion | flops 46995865600 | bytes 102236160 | tf_op jit(solution)/shard_map/dot_general | solution.py:11
  214.2 55.6 %convolution_convert_fusion = bf16[640,7168]{1,0:T(8,128)(2,1)} fusion(bf16[640,5120]{1,0:T(8,128)(2,1)} %multiply_convert_fusion, bf16[5120,7168]{1,0:T(8,128)(2,1)} %param.7), kind=kOutput, calls=%fused_computation.1 | convolution fusion | flops 46980792320 | bytes 89128960 | tf_op jit(solution)/shard_map/dot_general | solution.py:13
  269.8 0.1 reduce-scatter.2.cloned.1.call-update
  269.9 83.9 %reduce-scatter.2.cloned.1.call-done = bf16[160,7168]{1,0:T(8,128)(2,1)} async-done(((bf16[640,7168]{1,0:T(8,128)(2,1)}), bf16[160,7168]{1,0:T(8,128)(2,1)}) %reduce-scatter.2.cloned.1.call-update) | async-done | bytes 2293776 | tf_op jit(solution)/shard_map/reduce_scatter | solution.py:14
Async XLA Ops:
  6.5 91.2 %all-gather.2.cloned.1.call-start = ((), (), s32[]{:S(2)}) async-start(), calls=%async_computation.1 | async-start | bytes 11468800 | tf_op jit(solution)/shard_map/all_gather | solution.py:9
  7.3 346.5 %reduce-scatter.2.cloned.1.call-start = ((), (), s32[]{:S(2)}) async-start(), calls=%async_computation.2 | async-start | bytes 11468800 | tf_op jit(solution)/shard_map/reduce_scatter | solution.py:14
Sparse Core Ops, SparseCore 0:
  8.9 88.7 all-gather.1
  270.0 83.7 reduce-scatter.1
where the time goes:
time: 361 us
  waiting for transfers between devices  175 us (48%)
  matrix products  172 us (48%)
  between operations  13.4 us (4%)
    all_gather x1, waiting for transfers between devices, step(): rows = lax.all_gather(x, 'tp', axis=0, tiled=True)  90.4 us
    reduce_scatter x1, waiting for transfers between devices, step(): return lax.psum_scatter(term, 'tp', scatter_dimension=0, tiled=True)  83.9 us
    dot_general x1, matrix products, step(): up = jnp.dot(rows, w_up, preferred_element_type=jnp.float32)  59 us
    dot_general x1, matrix products, step(): gate = jnp.dot(rows, w_gate, preferred_element_type=jnp.float32)  57.5 us
    dot_general x1, matrix products, step(): jnp.dot(hidden, w_down, preferred_element_type=jnp.float32)  55.6 us
  transfers between devices with their start and end apart: 2, of which 2 were waited for; matrix products, arithmetic and copies ran while one was open for 0% of the time, Pallas kernels for 0%

commit v1 on v0

v1 whole, which is shorter than its diff:
```python
import functools

import jax
import jax.numpy as jnp
from jax import lax
from jax.experimental import pallas as pl
from jax.experimental.pallas import tpu as pltpu
from jax.sharding import PartitionSpec as P

F32 = jnp.float32
BF16 = jnp.bfloat16
KC = 1024
NU = 512
RING = 20
COMM = True


def _kernel(
    x_ref, wg_ref, wu_ref, wd_ref, out_ref,
    xbuf, acc_g, acc_u, hid, wbuf, thru, own, obuf, rfar, rsum, rdir, sfar, ssum, sdir,
    wsem, xsem, osem, ag_send, agf_send, ag_recv, agf_recv, rs_send, far_recv, sum_recv, dir_recv,
):
    n = 4
    rows, dim = x_ref.shape
    r = rows // 2
    ff = wg_ref.shape[1]
    nk = dim // KC
    nb1 = ff // (2 * NU)
    kd = ff // KC
    npair = dim // (2 * NU)
    nt = 2 * npair
    me = lax.axis_index("tp")
    right, left = {"tp": lax.rem(me + 1, n)}, {"tp": lax.rem(me + n - 1, n)}
    mesh_id = pl.DeviceIdType.MESH

    def m(v, k):
        return pl.multiple_of(v, k)

    def put(ref, k, c, slot):
        pltpu.make_async_copy(
            ref.at[pl.ds(m(k * KC, KC), KC), pl.ds(m(c * NU, NU), NU)], wbuf.at[slot], wsem.at[slot]
        ).start()

    def start_up(h, kc, nb, j):
        slot = lax.rem(10 * h + 4 * nb + j, RING)
        put(wg_ref if j % 2 == 0 else wu_ref, kc, 2 * nb + j // 2, slot)

    def start_down(h, q):
        put(wd_ref, lax.rem(q, kd), q // kd, lax.rem(10 * h + q, RING))

    def await_slot(slot):
        pltpu.make_async_copy(wg_ref.at[pl.ds(0, KC), pl.ds(0, NU)], wbuf.at[slot], wsem.at[slot]).wait()

    def cut(k):
        return k // nk, pl.ds(m(lax.rem(k, nk) * KC, KC), KC)

    def ag_own(k, d):
        h, cols = cut(k)
        return pltpu.make_async_remote_copy(
            src_ref=x_ref.at[pl.ds(m(h * r, r), r), cols],
            dst_ref=xbuf.at[h, pl.ds((3 if d == 0 else 1) * r, r), cols],
            send_sem=ag_send.at[d], recv_sem=ag_recv.at[d, k],
            device_id=right if d == 0 else left, device_id_type=mesh_id)

    def ag_fwd(k, d):
        h = k // nk
        cols = pl.ds(m(lax.rem(k, nk) * KC + d * (KC // 2), KC // 2), KC // 2)
        return pltpu.make_async_remote_copy(
            src_ref=xbuf.at[h, pl.ds((3 if d == 0 else 1) * r, r), cols],
            dst_ref=xbuf.at[h, pl.ds(2 * r, r), cols],
            send_sem=agf_send.at[d], recv_sem=agf_recv.at[d, k],
            device_id=right if d == 0 else left, device_id_type=mesh_id)

    def ag_start(k):
        for d in range(2):
            ag_own(k, d).start()

    def ag_point(k, last=False):
        for d in range(2):
            ag_own(k, d).wait_recv()
            ag_fwd(k, d).start()
        if not last:
            ag_start(k + 2)

    def rs_copy(kind, h, t, c):
        src, dst, sem = ((sfar, rfar, far_recv), (ssum, rsum, sum_recv), (sdir, rdir, dir_recv))[kind]
        to_right = (c == 0) != (kind == 2)
        i = h * nt + t
        return pltpu.make_async_remote_copy(
            src_ref=src.at[t], dst_ref=dst.at[i], send_sem=rs_send.at[kind], recv_sem=sem.at[i],
            device_id=right if to_right else left, device_id_type=mesh_id)

    def rs_start(kind, h, p):
        for c in range(2):
            rs_copy(kind, h, 2 * p + c, c).start()

    def rs_pass(h, p):
        for c in range(2):
            t = 2 * p + c
            rs_copy(0, h, t, c).wait_recv()
            ssum[t] = (thru[t] + rfar[h * nt + t].astype(F32)).astype(BF16)
        rs_start(1, h, p)

    def rs_final(h, p):
        for c in range(2):
            t = 2 * p + c
            i = h * nt + t
            rs_copy(1, h, t, c).wait_recv()
            rs_copy(2, h, t, c).wait_recv()
            cols = pl.ds(m(t * NU, NU), NU)
            rws = pl.ds(m(h * r, r), r)
            obuf[rws, cols] = (own[t] + rsum[i].astype(F32) + rdir[i].astype(F32)).astype(BF16)
        cols = pl.ds(m(2 * p * NU, 2 * NU), 2 * NU)
        pltpu.make_async_copy(obuf.at[rws, cols], out_ref.at[rws, cols], osem).start()

    def rs_sent():
        for kind, buf in enumerate((sfar, ssum, sdir)):
            pltpu.make_async_copy(buf, buf, rs_send.at[kind]).wait()

    for nb in range(nb1):
        for j in range(4):
            start_up(0, 0, nb, j)
    for h in range(2):
        pltpu.make_async_copy(x_ref.at[pl.ds(h * r, r)], xbuf.at[h, pl.ds(0, r)], xsem.at[h]).start()
    if COMM:
        barrier = pltpu.get_barrier_semaphore()
        for d in (left, right):
            pl.semaphore_signal(barrier, inc=1, device_id=d, device_id_type=mesh_id)
        pl.semaphore_wait(barrier, 2)
        ag_start(0)
        ag_start(1)
        ag_point(0)
        ag_point(1)
    for h in range(2):
        pltpu.make_async_copy(x_ref.at[pl.ds(h * r, r)], xbuf.at[h, pl.ds(0, r)], xsem.at[h]).wait()

    def half(h, _):
        def up_body(kc, nb, first, last):
            for j in range(4):
                await_slot(lax.rem(10 * h + 4 * nb + j, RING))
            xk = xbuf[h, :, pl.ds(m(kc * KC, KC), KC)]
            for c in range(2):
                cols = pl.ds(m(nb * 2 * NU + c * NU, NU), NU)
                s0 = lax.rem(10 * h + 4 * nb + 2 * c, RING)
                s1 = lax.rem(10 * h + 4 * nb + 2 * c + 1, RING)
                g = jnp.dot(xk, wbuf[s0], preferred_element_type=F32)
                u = jnp.dot(xk, wbuf[s1], preferred_element_type=F32)
                if not first:
                    g = acc_g[:, cols] + g
                    u = acc_u[:, cols] + u
                if last:
                    hid[:, cols] = (jax.nn.silu(g) * u).astype(BF16)
                else:
                    acc_g[:, cols] = g
                    acc_u[:, cols] = u
            for j in range(4):
                if last:
                    start_down(h, 4 * nb + j)
                else:
                    start_up(h, kc + 1, nb, j)
            if COMM:
                b = kc * nb1 + nb

                @pl.when((h == 0) & (lax.rem(b, 4) == 2))
                def _():
                    ag_point(b // 4 + 2)

                @pl.when((h == 1) & (lax.rem(b, 4) == 0) & (b >= 4) & (b < 4 + 4 * npair))
                def _():
                    rs_pass(0, b // 4 - 1)

                @pl.when((h == 1) & (lax.rem(b, 4) == 2) & (b >= 10) & (b < 10 + 4 * npair))
                def _():
                    rs_final(0, (b - 10) // 4)

        def chunk(kc, first, last):
            if COMM:
                for d in range(2):
                    ag_fwd(h * nk + kc, d).wait_recv()

            def one(nb, _):
                up_body(kc, nb, first, last)
                return 0

            lax.fori_loop(0, nb1, one, 0)

        chunk(0, True, False)

        def mid(kc, _):
            chunk(kc, False, False)
            return 0

        lax.fori_loop(1, nk - 1, mid, 0)
        chunk(nk - 1, False, True)

        if COMM:
            @pl.when(h == 1)
            def _():
                rs_sent()

        def down(p, _):
            for i in range(2 * kd):
                await_slot(lax.rem(10 * h + 10 * p + i, RING))
            for c in range(2):
                t = 2 * p + c
                y = jnp.dot(hid[:, :KC], wbuf[lax.rem(10 * h + 10 * p + 5 * c, RING)], preferred_element_type=F32)
                for k in range(1, kd):
                    y += jnp.dot(hid[:, k * KC:(k + 1) * KC], wbuf[lax.rem(10 * h + 10 * p + 5 * c + k, RING)],
                                 preferred_element_type=F32)
                own[t] = y[:r]
                sfar[t] = y[2 * r:3 * r].astype(BF16)
                thru[t] = y[r:2 * r] if c == 0 else y[3 * r:]
                sdir[t] = (y[3 * r:] if c == 0 else y[r:2 * r]).astype(BF16)
            if COMM:
                rs_start(0, h, p)

            @pl.when(p < npair - 2)
            def _():
                for i in range(2 * kd):
                    start_down(h, 10 * (p + 2) + i)

            @pl.when((p >= npair - 2) & (h == 0))
            def _():
                for i in range(2 * kd):
                    q = 10 * (p - (npair - 2)) + i
                    slot = lax.rem(10 + q, RING)
                    put(wg_ref if i % 2 == 0 else wu_ref, 0, q // 2, slot)

            if COMM:
                @pl.when((h == 0) | (p == 0))
                def _():
                    rs_start(2, h, p)

                @pl.when((h == 0) & (p == 0))
                def _():
                    ag_point(11)

                @pl.when((h == 0) & ((p == 2) | (p == 3)))
                def _():
                    ag_point(10 + p, last=True)

                @pl.when((h == 1) & (p >= 1))
                def _():
                    rs_pass(1, p - 1)
            return 0

        lax.fori_loop(0, npair, down, 0)
        return 0

    lax.fori_loop(0, 2, half, 0)

    if COMM:
        rs_start(2, 1, 1)
        rs_start(2, 1, 2)
        rs_pass(1, npair - 1)
        for p in range(3, npair):
            rs_start(2, 1, p)

        def fin(p, _):
            rs_final(1, p)
            return 0

        lax.fori_loop(0, npair, fin, 0)
        rs_sent()
        for d in range(2):
            pltpu.make_async_copy(x_ref, x_ref, ag_send.at[d]).wait()
            half_x = x_ref.at[:, pl.ds(0, dim // 2)]
            pltpu.make_async_copy(half_x, half_x, agf_send.at[d]).wait()
        pltpu.make_async_copy(obuf, out_ref, osem).wait()
    else:
        obuf[...] = jnp.zeros_like(obuf)
        obuf[:r, :NU] = own[0].astype(BF16)
        c = pltpu.make_async_copy(obuf, out_ref, osem)
        c.start()
        c.wait()


def solution(mesh):
    def step(x, w_gate, w_up, w_down):
        rows, dim = x.shape
        ff = w_gate.shape[1]
        r, nt = rows // 2, dim // NU
        n = mesh.shape["tp"]
        nag = 2 * (dim // KC)
        vm, dma = pltpu.VMEM, pltpu.SemaphoreType.DMA
        return pl.pallas_call(
            _kernel,
            out_shape=jax.ShapeDtypeStruct((rows, dim), BF16),
            in_specs=[pl.BlockSpec(memory_space=pl.ANY)] * 4,
            out_specs=pl.BlockSpec(memory_space=pl.ANY),
            scratch_shapes=[
                vm((2, n * r, dim), BF16),
                vm((n * r, ff), F32),
                vm((n * r, ff), F32),
                vm((n * r, ff), BF16),
                vm((RING, KC, NU), BF16),
                vm((nt, r, NU), F32),
                vm((nt, r, NU), F32),
                vm((rows, dim), BF16),
                vm((2 * nt, r, NU), BF16),
                vm((2 * nt, r, NU), BF16),
                vm((2 * nt, r, NU), BF16),
                vm((nt, r, NU), BF16),
                vm((nt, r, NU), BF16),
                vm((nt, r, NU), BF16),
                dma((RING,)),
                dma((2,)),
                dma,
                dma((2,)),
                dma((2,)),
                dma((2, nag)),
                dma((2, nag)),
                dma((3,)),
                dma((2 * nt,)),
                dma((2 * nt,)),
                dma((2 * nt,)),
            ],
            compiler_params=pltpu.CompilerParams(
                collective_id=0 if COMM else None, has_side_effects=True, vmem_limit_bytes=67043328),
        )(x, w_gate, w_up, w_down)

    return jax.shard_map(
        step, mesh=mesh,
        in_specs=(P(("dp", "tp"), None), P(None, "tp"), P(None, "tp"), P("tp", None)),
        out_specs=P(("dp", "tp"), None), check_vma=False)
```

time: 361 us -> 207 us (0.57)
  Pallas kernels: 0 us -> 203 us
  waiting for transfers between devices: 175 us -> 0 us
  matrix products: 172 us -> 0 us
  between operations: 13.4 us -> 0.01 us
    pallas_call x0 -> x1, Pallas kernels: none -> 203 us  [step(): pl.pallas_call(_kernel, out_shape=jax.ShapeDtypeStruct((rows, dim), BF16)...]
    dot_general x3 -> x0, matrix products: 172 us -> none  [the longest x1 59 us: step(): up = jnp.dot(rows, w_up, preferred_element_type=jnp.float32)]
    all_gather x1 -> x0, waiting for transfers between devices: 90.4 us -> none  [step(): rows = lax.all_gather(x, 'tp', axis=0, tiled=True)]
    reduce_scatter x1 -> x0, waiting for transfers between devices: 83.9 us -> none  [step(): return lax.psum_scatter(term, 'tp', scatter_dimension=0, tiled=True)]
  transfers between devices with their start and end apart: 2 -> 0, of which waited for: 2 -> 0; matrix products, arithmetic and copies ran while one was open for 0% -> 0% of each run, Pallas kernels for 0% -> 0%
where the time goes in v1:
time: 207 us
  Pallas kernels  203 us (98%)
  local copies, waits for them, and re-layouts  3.18 us (2%)
    pallas_call x1, Pallas kernels, step(): pl.pallas_call(_kernel, out_shape=jax.ShapeDtypeStruct((rows, dim), BF16)...  203 us

profile of v1, /device:TPU:112, one launch (start us, length us, event | category | flops | bytes accessed | tf_op | source)
XLA Modules:
  0.0 206.5 jit_solution(16162567737684377350)
XLA Ops:
  0.0 203.4 %shard_map.46 = bf16[160,7168]{1,0:T(8,128)(2,1)} custom-call(bf16[160,7168]{1,0:T(8,128)(2,1)} %x_ref.1, bf16[7168,5120]{1,0:T(8,128)(2,1)} %wg_ref.1, bf16[7168,5120]{1,0:T(8,128)(2,1)} %wu_ref.1, bf16[5120,7168]{1,0:T(8,128)(2,1)} %wd_ref.1), custom_call_target="tpu_custom_call" | custom-call | tf_op jit(solution)/shard_map/pallas_call | solution.py:286
  203.4 3.2 %copy.6 = bf16[160,7168]{1,0:T(8,128)(2,1)} copy(bf16[160,7168]{1,0:T(8,128)(2,1)} %shard_map.46) | data formatting | bytes 4587520

commit v2 on v0

v2 whole, which is shorter than its diff:
```python
import jax
import jax.numpy as jnp
from jax import lax
from jax.experimental import pallas as pl
from jax.experimental.pallas import tpu as pltpu
from jax.sharding import PartitionSpec as P

F32 = jnp.float32
BF16 = jnp.bfloat16
KC = 1024
NU = 512
BODY = 10
RING = 2 * BODY
LAG = 4
COMM = True
DMA = True


def _kernel(
    x_ref, wg_ref, wu_ref, wd_ref, out_ref,
    xbuf, acc_g, acc_u, hid, wbuf, thru, own, rfar, rsum, rdir, sfar, ssum, sdir,
    wsem, xsem, ag_send, agf_send, ag_recv, agf_recv, rs_send, far_recv, sum_recv, dir_recv,
):
    n = 4
    rows, dim = x_ref.shape
    r = rows // 2
    ff = wg_ref.shape[1]
    nk = dim // KC
    nc = BODY // 2
    kd = ff // KC
    npair = dim // (2 * NU)
    nt = 2 * npair
    npc = dim // NU
    me = lax.axis_index("tp")
    right, left = {"tp": lax.rem(me + 1, n)}, {"tp": lax.rem(me + n - 1, n)}
    mesh_id = pl.DeviceIdType.MESH

    def m(v, k):
        return v if isinstance(v, int) else pl.multiple_of(v, k)

    def put(ref, k, c, slot):
        if DMA:
            pltpu.make_async_copy(
                ref.at[pl.ds(m(k * KC, KC), KC), pl.ds(m(c * NU, NU), NU)], wbuf.at[slot], wsem.at[slot]
            ).start()

    def put_up(h, kc, i, c):
        base = BODY * lax.rem(i + h, 2)
        for j, ref in enumerate((wg_ref, wu_ref)):
            put(ref, kc, nc * i + c, base + 2 * c + j)

    def put_down(h, p, idx):
        put(wd_ref, idx % kd, 2 * p + idx // kd, BODY * lax.rem(p + h, 2) + idx)

    def await_slot(slot):
        if DMA:
            pltpu.make_async_copy(wg_ref.at[pl.ds(0, KC), pl.ds(0, NU)], wbuf.at[slot], wsem.at[slot]).wait()

    def ag_own(s, d):
        h = s // npc
        cols = pl.ds(m((s % npc) * NU, NU), NU)
        return pltpu.make_async_remote_copy(
            src_ref=x_ref.at[pl.ds(m(h * r, r), r), cols],
            dst_ref=xbuf.at[h, pl.ds((3 if d == 0 else 1) * r, r), cols],
            send_sem=ag_send.at[d], recv_sem=ag_recv.at[d, s],
            device_id=right if d == 0 else left, device_id_type=mesh_id)

    def ag_fwd(s, d):
        h = s // npc
        cols = pl.ds(m((s % npc) * NU + d * (NU // 2), NU // 2), NU // 2)
        return pltpu.make_async_remote_copy(
            src_ref=xbuf.at[h, pl.ds((3 if d == 0 else 1) * r, r), cols],
            dst_ref=xbuf.at[h, pl.ds(2 * r, r), cols],
            send_sem=agf_send.at[d], recv_sem=agf_recv.at[d, s],
            device_id=right if d == 0 else left, device_id_type=mesh_id)

    def ag_start(s):
        if COMM:
            for d in range(2):
                ag_own(s, d).start()

    def ag_pass(s):
        if COMM:
            for d in range(2):
                ag_own(s, d).wait_recv()
                ag_fwd(s, d).start()

    def ag_done(s):
        if COMM:
            for d in range(2):
                ag_fwd(s, d).wait_recv()

    FAR, SUM, DIR = range(3)

    def rs_copy(kind, h, p, c):
        src, dst, sem = ((sfar, rfar, far_recv), (ssum, rsum, sum_recv), (sdir, rdir, dir_recv))[kind]
        to_right = (c == 0) != (kind == DIR)
        t = 2 * p + c
        i = h * nt + t
        return pltpu.make_async_remote_copy(
            src_ref=src.at[t], dst_ref=dst.at[i], send_sem=rs_send.at[kind], recv_sem=sem.at[i],
            device_id=right if to_right else left, device_id_type=mesh_id)

    def rs_start(kind, h, p, c):
        if COMM:
            rs_copy(kind, h, p, c).start()

    def rs_pass(h, p, c):
        t = 2 * p + c
        rs_copy(FAR, h, p, c).wait_recv()
        ssum[t] = (thru[t] + rfar[h * nt + t].astype(F32)).astype(BF16)
        rs_start(SUM, h, p, c)

    def rs_final(h, p):
        for c in range(2):
            t = 2 * p + c
            i = h * nt + t
            rs_copy(SUM, h, p, c).wait_recv()
            rs_copy(DIR, h, p, c).wait_recv()
            out_ref[pl.ds(h * r, r), pl.ds(m(t * NU, NU), NU)] = (
                own[t] + rsum[i].astype(F32) + rdir[i].astype(F32)).astype(BF16)

    def rs_sent():
        for kind, buf in enumerate((sfar, ssum, sdir)):
            pltpu.make_async_copy(buf, buf, rs_send.at[kind]).wait()

    if COMM:
        barrier = pltpu.get_barrier_semaphore()
        for d in (left, right):
            pl.semaphore_signal(barrier, inc=1, device_id=d, device_id_type=mesh_id)
    for c in range(nc):
        put_up(0, 0, 0, c)
    for h in range(2):
        pltpu.make_async_copy(x_ref.at[pl.ds(h * r, r)], xbuf.at[h, pl.ds(0, r)], xsem.at[h]).start()
    if COMM:
        pl.semaphore_wait(barrier, 2)
    ag_start(0)
    ag_start(1)
    for c in range(nc):
        put_up(0, 0, 1, c)
    ag_pass(0)
    ag_start(2)
    ag_pass(1)
    ag_start(3)
    for h in range(2):
        pltpu.make_async_copy(x_ref.at[pl.ds(h * r, r)], xbuf.at[h, pl.ds(0, r)], xsem.at[h]).wait()

    def up_step(h, kc, i, depth, first, last, refill, wait):
        base = BODY * lax.rem(i + h, 2)
        off, size = depth
        xk = xbuf[h, :, pl.ds(m(kc * KC + off, size), size)]

        def ready(c):
            if wait and c < nc:
                await_slot(base + 2 * c)
                await_slot(base + 2 * c + 1)

        def refill_tile(c):
            if refill == "up":
                put_up(h, kc + 1, i, c)
            elif refill == "down":
                for j in range(2):
                    put_down(h, i, 2 * c + j)

        for c in range(nc):
            ready(c)
        for c in range(nc):
            cols = pl.ds(m((nc * i + c) * NU, NU), NU)
            g = jnp.dot(xk, wbuf[base + 2 * c, pl.ds(off, size)], preferred_element_type=F32)
            u = jnp.dot(xk, wbuf[base + 2 * c + 1, pl.ds(off, size)], preferred_element_type=F32)
            if not first:
                g = acc_g[:, cols] + g
                u = acc_u[:, cols] + u
            if last:
                hid[:, cols] = (jax.nn.silu(g) * u).astype(BF16)
            else:
                acc_g[:, cols] = g
                acc_u[:, cols] = u
            if refill and c >= 1:
                refill_tile(c - 1)
        if refill:
            refill_tile(nc - 1)

    def loop(lo, hi, body):
        def step(i, _):
            body(i)
            return 0
        lax.fori_loop(lo, hi, step, 0)

    def rs_between(b):
        if not COMM:
            return

        @pl.when((b >= 1) & (b <= npair))
        def _():
            for c in range(2):
                rs_pass(0, b - 1, c)

        @pl.when((b >= 2 * nk - npair) & (b < 2 * nk))
        def _():
            rs_final(0, b - (2 * nk - npair))

    for h in range(2):
        if h == 0:
            ag_done(0)

            def first_a(i):
                up_step(0, 0, i, (0, KC // 2), True, False, None, True)
                ag_pass(2 + i)
                ag_start(4 + i)
            loop(0, 2, first_a)
            ag_done(1)

            def first_b(i):
                up_step(0, 0, i, (KC // 2, KC // 2), False, False, "up", False)
                ag_start(6 + i)
            loop(0, 2, first_b)

            def mid(kc, last=False):
                ag_done(2 * kc)
                ag_done(2 * kc + 1)
                q = 4 + 3 * (kc - 1)

                def one(i):
                    up_step(0, kc, i, (0, KC), False, last, "down" if last else "up", True)

                    @pl.when(i == 0)
                    def _():
                        ag_pass(q)
                        ag_pass(q + 1)
                        ag_start(q + LAG)
                        ag_start(q + LAG + 1)

                    @pl.when(i == 1)
                    def _():
                        ag_pass(q + 2)
                        ag_start(q + LAG + 2)
                loop(0, 2, one)
            loop(1, nk - 1, mid)
            mid(nk - 1, True)
            passed = 4 + 3 * (nk - 1)
        else:
            def chunk(kc, first, last):
                ag_done(npc + 2 * kc)
                ag_done(npc + 2 * kc + 1)

                def one(i):
                    up_step(1, kc, i, (0, KC), first, last, "down" if last else "up", True)
                    rs_between(2 * kc + i)
                loop(0, 2, one)

            chunk(0, True, False)
            loop(1, nk - 1, lambda kc: chunk(kc, False, False))
            chunk(nk - 1, False, True)
            if COMM:
                rs_sent()

        def down(p, tail):
            base = BODY * lax.rem(p + h, 2)
            for idx in range(kd):
                await_slot(base + idx)
            for c in range(2):
                if c == 0:
                    for idx in range(kd, 2 * kd):
                        await_slot(base + idx)
                y = None
                for k in range(kd):
                    z = jnp.dot(hid[:, k * KC:(k + 1) * KC], wbuf[base + c * kd + k], preferred_element_type=F32)
                    y = z if y is None else y + z
                t = 2 * p + c
                own[t] = y[:r]
                sfar[t] = y[2 * r:3 * r].astype(BF16)
                thru[t] = y[r:2 * r] if c == 0 else y[3 * r:]
                sdir[t] = (y[3 * r:] if c == 0 else y[r:2 * r]).astype(BF16)
                rs_start(FAR, h, p, c)
                if h == 0 or not tail:
                    rs_start(DIR, h, p, c)
                for idx in range(c * kd, (c + 1) * kd):
                    if not tail:
                        put_down(h, p + 2, idx)
                    elif h == 0:
                        put((wg_ref, wu_ref)[idx % 2], 0, nc * (p - (npair - 2)) + idx // 2,
                            BODY * lax.rem(p - (npair - 2) + 1, 2) + idx)
            if not COMM:
                return
            if h == 0:
                s = passed + p

                @pl.when(s < 2 * npc)
                def _():
                    ag_pass(s)

                @pl.when(s + LAG < 2 * npc)
                def _():
                    ag_start(s + LAG)
            else:
                @pl.when(p >= 1)
                def _():
                    rs_pass(1, p - 1, 0)

                @pl.when(p >= 2)
                def _():
                    rs_pass(1, p - 2, 1)

        loop(0, npair - 2, lambda p: down(p, False))
        loop(npair - 2, npair, lambda p: down(p, True))

    if COMM:
        rs_pass(1, npair - 2, 1)
        for c in range(2):
            rs_start(DIR, 1, npair - 2, c)
        for c in range(2):
            rs_pass(1, npair - 1, c)
        for c in range(2):
            rs_start(DIR, 1, npair - 1, c)
        loop(0, npair, lambda p: rs_final(1, p))
        rs_sent()
        for d in range(2):
            pltpu.make_async_copy(x_ref, x_ref, ag_send.at[d]).wait()
            half_x = x_ref.at[:, pl.ds(0, dim // 2)]
            pltpu.make_async_copy(half_x, half_x, agf_send.at[d]).wait()
    else:
        out_ref[:r, :NU] = own[0].astype(BF16)


def solution(mesh):
    def step(x, w_gate, w_up, w_down):
        rows, dim = x.shape
        ff = w_gate.shape[1]
        r, nt = rows // 2, dim // NU
        n = mesh.shape["tp"]
        vm, dma = pltpu.VMEM, pltpu.SemaphoreType.DMA
        return pl.pallas_call(
            _kernel,
            out_shape=pltpu.VMEM((rows, dim), BF16),
            in_specs=[pl.BlockSpec(memory_space=pl.ANY)] * 4,
            out_specs=pl.BlockSpec(memory_space=pltpu.VMEM),
            scratch_shapes=[
                vm((2, n * r, dim), BF16),
                vm((n * r, ff), F32),
                vm((n * r, ff), F32),
                vm((n * r, ff), BF16),
                vm((RING, KC, NU), BF16),
                vm((nt, r, NU), F32),
                vm((nt, r, NU), F32),
                vm((2 * nt, r, NU), BF16),
                vm((2 * nt, r, NU), BF16),
                vm((2 * nt, r, NU), BF16),
                vm((nt, r, NU), BF16),
                vm((nt, r, NU), BF16),
                vm((nt, r, NU), BF16),
                dma((RING,)),
                dma((2,)),
                dma((2,)),
                dma((2,)),
                dma((2, 2 * nt)),
                dma((2, 2 * nt)),
                dma((3,)),
                dma((2 * nt,)),
                dma((2 * nt,)),
                dma((2 * nt,)),
            ],
            compiler_params=pltpu.CompilerParams(
                collective_id=0 if COMM else None, has_side_effects=True, vmem_limit_bytes=67043328 - 2400000),
        )(x, w_gate, w_up, w_down)

    return jax.shard_map(
        step, mesh=mesh,
        in_specs=(P(("dp", "tp"), None), P(None, "tp"), P(None, "tp"), P("tp", None)),
        out_specs=P(("dp", "tp"), None), check_vma=False)
```

time: 361 us -> 190 us (0.53)
  Pallas kernels: 0 us -> 188 us
  waiting for transfers between devices: 175 us -> 0 us
  matrix products: 172 us -> 0 us
  between operations: 13.4 us -> 0.01 us
    pallas_call x0 -> x1, Pallas kernels: none -> 188 us  [step(): pl.pallas_call(_kernel, out_shape=pltpu.VMEM((rows, dim), BF16), in_specs...]
    dot_general x3 -> x0, matrix products: 172 us -> none  [the longest x1 59 us: step(): up = jnp.dot(rows, w_up, preferred_element_type=jnp.float32)]
    all_gather x1 -> x0, waiting for transfers between devices: 90.4 us -> none  [step(): rows = lax.all_gather(x, 'tp', axis=0, tiled=True)]
    reduce_scatter x1 -> x0, waiting for transfers between devices: 83.9 us -> none  [step(): return lax.psum_scatter(term, 'tp', scatter_dimension=0, tiled=True)]
  transfers between devices with their start and end apart: 2 -> 0, of which waited for: 2 -> 0; matrix products, arithmetic and copies ran while one was open for 0% -> 0% of each run, Pallas kernels for 0% -> 0%
where the time goes in v2:
time: 190 us
  Pallas kernels  188 us (99%)
    pallas_call x1, Pallas kernels, step(): pl.pallas_call(_kernel, out_shape=pltpu.VMEM((rows, dim), BF16), in_specs...  188 us

profile of v2, /device:TPU:112, one launch (start us, length us, event | category | flops | bytes accessed | tf_op | source)
XLA Modules:
  0.0 189.9 jit_solution(5330433569869986048)
XLA Ops:
  0.0 188.5 %shard_map.46 = bf16[160,7168]{1,0:T(8,128)(2,1)S(1)} custom-call(bf16[160,7168]{1,0:T(8,128)(2,1)} %x_ref.1, bf16[7168,5120]{1,0:T(8,128)(2,1)} %wg_ref.1, bf16[7168,5120]{1,0:T(8,128)(2,1)} %wu_ref.1, bf16[5120,7168]{1,0:T(8,128)(2,1)} %wd_ref.1), custom_call_target="tpu_custom_call" | custom-call | tf_op jit(solution)/shard_map/pallas_call | solution.py:333
  188.5 1.4 copy.6

commit v3 on v2

v3 whole, which is shorter than its diff:
```python
import jax
import jax.numpy as jnp
from jax import lax
from jax.experimental import pallas as pl
from jax.experimental.pallas import tpu as pltpu
from jax.sharding import PartitionSpec as P

F32 = jnp.float32
BF16 = jnp.bfloat16
KC = 1024
NU = 512
BODY = 10
RING = 2 * BODY


def _kernel(
    x_ref, wg_ref, wu_ref, wd_ref, out_ref,
    xbuf, acc_g, acc_u, hid, wbuf, thru, own, rfar, rsum, rdir, sfar, ssum, sdir,
    wsem, xsem, ag_send, agf_send, ag_recv, agf_recv, rs_send, far_recv, sum_recv, dir_recv,
):
    n = 4
    rows, dim = x_ref.shape
    r = rows // 2
    ff = wg_ref.shape[1]
    nk = dim // KC
    nc = BODY // 2
    kd = ff // KC
    npair = dim // (2 * NU)
    nt = 2 * npair
    nw = nk + 2
    npc = nw + nk
    me = lax.axis_index("tp")
    right, left = {"tp": lax.rem(me + 1, n)}, {"tp": lax.rem(me + n - 1, n)}
    mesh_id = pl.DeviceIdType.MESH

    def m(v, k):
        return v if isinstance(v, int) else pl.multiple_of(v, k)

    def put(ref, k, c, side, idx):
        pltpu.make_async_copy(
            ref.at[pl.ds(m(k * KC, KC), KC), pl.ds(m(c * NU, NU), NU)], wbuf.at[side * BODY + idx], wsem.at[side]
        ).start()

    def put_up(h, kc, i, c):
        for j, ref in enumerate((wg_ref, wu_ref)):
            put(ref, kc, nc * i + c, lax.rem(i + h, 2), 2 * c + j)

    def put_down(h, p, idx):
        put(wd_ref, idx % kd, 2 * p + idx // kd, lax.rem(p + h, 2), idx)

    def await_tiles(side):
        tiles = wbuf.at[pl.ds(side * BODY, BODY)]
        pltpu.make_async_copy(tiles, tiles, wsem.at[side]).wait()

    def piece(s):
        if isinstance(s, int) and s < 4:
            return 0, s * NU, NU
        h = s // nw
        return h, (s - 2 - nk * h) * KC, KC

    def ag_own(s, d):
        h, c0, width = piece(s)
        cols = pl.ds(m(c0, NU), width)
        return pltpu.make_async_remote_copy(
            src_ref=x_ref.at[pl.ds(m(h * r, r), r), cols],
            dst_ref=xbuf.at[h, pl.ds((3 if d == 0 else 1) * r, r), cols],
            send_sem=ag_send.at[d], recv_sem=ag_recv.at[d, s],
            device_id=right if d == 0 else left, device_id_type=mesh_id)

    def ag_fwd(s, d):
        h, c0, width = piece(s)
        cols = pl.ds(m(c0 + d * (width // 2), NU // 2), width // 2)
        return pltpu.make_async_remote_copy(
            src_ref=xbuf.at[h, pl.ds((3 if d == 0 else 1) * r, r), cols],
            dst_ref=xbuf.at[h, pl.ds(2 * r, r), cols],
            send_sem=agf_send.at[d], recv_sem=agf_recv.at[d, s],
            device_id=right if d == 0 else left, device_id_type=mesh_id)

    def ag_start(s):
        for d in range(2):
            ag_own(s, d).start()

    def ag_pass(s):
        for d in range(2):
            ag_own(s, d).wait_recv()
            ag_fwd(s, d).start()

    def ag_done(s):
        for d in range(2):
            ag_fwd(s, d).wait_recv()

    FAR, SUM, DIR = range(3)

    def rs_copy(kind, h, p, c):
        src, dst, sem = ((sfar, rfar, far_recv), (ssum, rsum, sum_recv), (sdir, rdir, dir_recv))[kind]
        step = lax.rem(c, 2) if kind != DIR else 1 - lax.rem(c, 2)
        to = {"tp": lax.rem(me + 1 + (n - 2) * step, n)}
        t = 2 * p + c
        i = h * nt + t
        return pltpu.make_async_remote_copy(
            src_ref=src.at[t], dst_ref=dst.at[i], send_sem=rs_send.at[kind], recv_sem=sem.at[i],
            device_id=to, device_id_type=mesh_id)

    def rs_start(kind, h, p, c):
        rs_copy(kind, h, p, c).start()

    def rs_pass(h, p, c):
        t = 2 * p + c
        rs_copy(FAR, h, p, c).wait_recv()
        ssum[t] = (thru[t] + rfar[h * nt + t].astype(F32)).astype(BF16)
        rs_start(SUM, h, p, c)

    def put_own(h, p, c, value):
        if h == 0:
            own[2 * p + c] = value
        else:
            (acc_g, acc_u)[c][:r, pl.ds(m(p * NU, NU), NU)] = value

    def get_own(h, p, c):
        return own[2 * p + c] if h == 0 else (acc_g, acc_u)[c][:r, pl.ds(m(p * NU, NU), NU)]

    def rs_final(h, p):
        for c in range(2):
            t = 2 * p + c
            i = h * nt + t
            rs_copy(SUM, h, p, c).wait_recv()
            rs_copy(DIR, h, p, c).wait_recv()
            out_ref[pl.ds(h * r, r), pl.ds(m(t * NU, NU), NU)] = (
                get_own(h, p, c) + rsum[i].astype(F32) + rdir[i].astype(F32)).astype(BF16)

    def rs_sent(*kinds):
        for kind in kinds:
            buf = (sfar, ssum, sdir)[kind]
            pltpu.make_async_copy(buf, buf, rs_send.at[kind]).wait()

    barrier = pltpu.get_barrier_semaphore()
    for d in (left, right):
        pl.semaphore_signal(barrier, inc=1, device_id=d, device_id_type=mesh_id)
    for h in range(2):
        pltpu.make_async_copy(x_ref.at[pl.ds(h * r, r)], xbuf.at[h, pl.ds(0, r)], xsem.at[h]).start()
    pl.semaphore_wait(barrier, 2)
    ag_start(0)
    ag_start(1)
    for c in range(nc):
        put_up(0, 0, 0, c)
    ag_pass(0)
    ag_start(2)
    for c in range(nc):
        put_up(0, 0, 1, c)
    ag_pass(1)
    ag_start(3)
    for h in range(2):
        pltpu.make_async_copy(x_ref.at[pl.ds(h * r, r)], xbuf.at[h, pl.ds(0, r)], xsem.at[h]).wait()

    def up_step(h, kc, i, depth, first, last, refill, wait, tile=None):
        base = BODY * lax.rem(i + h, 2)
        off, size = depth
        xk = xbuf[h, :, pl.ds(m(kc * KC + off, size), size)]

        def refill_tile(c):
            if refill == "up":
                put_up(h, kc + 1, i, c)
            elif refill == "down":
                for j in range(2):
                    put_down(h, i, 2 * c + j)

        if wait:
            await_tiles(lax.rem(i + h, 2))
        if tile is not None:
            rs_copy(FAR, 0, 0, tile).wait_recv()
        for c in range(nc):
            cols = pl.ds(m((nc * i + c) * NU, NU), NU)
            g = jnp.dot(xk, wbuf[base + 2 * c, pl.ds(off, size)], preferred_element_type=F32)
            u = jnp.dot(xk, wbuf[base + 2 * c + 1, pl.ds(off, size)], preferred_element_type=F32)
            if not first:
                g = acc_g[:, cols] + g
                u = acc_u[:, cols] + u
            if last:
                hid[:, cols] = (jax.nn.silu(g) * u).astype(BF16)
            else:
                acc_g[:, cols] = g
                acc_u[:, cols] = u
            if tile is not None and c == 1:
                ssum[tile] = (thru[tile] + rfar[tile].astype(F32)).astype(BF16)
            if refill and c >= 1:
                refill_tile(c - 1)
        if refill:
            refill_tile(nc - 1)
        if tile is not None:
            rs_copy(SUM, 0, 0, tile).start()

    def loop(lo, hi, body):
        def step(i, _):
            body(i)
            return 0
        lax.fori_loop(lo, hi, step, 0)

    for h in range(2):
        if h == 0:
            ag_done(0)

            def first_a(i):
                up_step(0, 0, i, (0, KC // 2), True, False, None, True)

                @pl.when(i == 0)
                def _():
                    ag_pass(2)
                    ag_start(4)

                @pl.when(i == 1)
                def _():
                    ag_pass(3)
            loop(0, 2, first_a)
            ag_done(1)

            def first_b(i):
                up_step(0, 0, i, (KC // 2, KC // 2), False, False, "up", False)

                @pl.when(i == 0)
                def _():
                    ag_start(5)
            loop(0, 2, first_b)
            ag_done(2)
            ag_done(3)

            def mid(kc, last=False):
                if last or not isinstance(kc, int):
                    @pl.when(kc > 1)
                    def _():
                        ag_done(kc + 2)

                def one(i):
                    up_step(0, kc, i, (0, KC), False, last, "down" if last else "up", True)
                    j = 2 * (kc - 1) + i
                    s = 4 + 2 * (j // 3) + lax.rem(j, 3)

                    @pl.when(lax.rem(j, 3) < 2)
                    def _():
                        ag_pass(s)
                        ag_start(s + 2)
                loop(0, 2, one)
            loop(1, nk - 1, mid)
            mid(jnp.int32(nk - 1), True)
            passed = 4 + 2 * (2 * (nk - 1) // 3)
        else:
            def chunk(kc, first, last):
                ag_done(nw + kc)

                def one(i):
                    up_step(1, kc, i, (0, KC), first, last, "down" if last else "up", True, tile=2 * kc + i)
                loop(0, 2, one)

            chunk(0, True, False)
            loop(1, nk - 1, lambda kc: chunk(kc, False, False))
            chunk(nk - 1, False, True)
            rs_sent(FAR, DIR)

        def down(p, tail):
            base = BODY * lax.rem(p + h, 2)
            await_tiles(lax.rem(p + h, 2))
            for c in range(2):
                y = None
                for k in range(kd):
                    z = jnp.dot(hid[:, k * KC:(k + 1) * KC], wbuf[base + c * kd + k], preferred_element_type=F32)
                    y = z if y is None else y + z
                t = 2 * p + c
                put_own(h, p, c, y[:r])
                sfar[t] = y[2 * r:3 * r].astype(BF16)
                thru[t] = y[r:2 * r] if c == 0 else y[3 * r:]
                sdir[t] = (y[3 * r:] if c == 0 else y[r:2 * r]).astype(BF16)
                rs_start(FAR, h, p, c)
                if h == 0 or not tail:
                    rs_start(DIR, h, p, c)
                for idx in range(c * kd, (c + 1) * kd):
                    if not tail:
                        put_down(h, p + 2, idx)
                    elif h == 0:
                        put((wg_ref, wu_ref)[idx % 2], 0, nc * (p - (npair - 2)) + idx // 2,
                            lax.rem(p - (npair - 2) + 1, 2), idx)
            if h == 0:
                @pl.when(p < 2)
                def _():
                    ag_pass(passed + p)
                    ag_start(passed + p + 2)

                @pl.when((p == 3) | (p == 5))
                def _():
                    ag_pass(passed + 2 + (p - 3) // 2)
            else:
                @pl.when(p == 1)
                def _():
                    rs_sent(SUM)

                @pl.when(p >= 1)
                def _():
                    rs_pass(1, p - 1, 0)

                @pl.when(p >= 2)
                def _():
                    rs_pass(1, p - 2, 1)

        loop(0, npair - 2, lambda p: down(p, False))
        loop(npair - 2, npair, lambda p: down(p, True))

    rs_pass(1, npair - 2, 1)
    for c in range(2):
        rs_start(DIR, 1, npair - 2, c)
    loop(0, npair, lambda p: rs_final(0, p))
    for c in range(2):
        rs_pass(1, npair - 1, c)
    for c in range(2):
        rs_start(DIR, 1, npair - 1, c)
    loop(0, npair, lambda p: rs_final(1, p))
    rs_sent(FAR, SUM, DIR)
    for d in range(2):
        pltpu.make_async_copy(x_ref, x_ref, ag_send.at[d]).wait()
        half_x = x_ref.at[:, pl.ds(0, dim // 2)]
        pltpu.make_async_copy(half_x, half_x, agf_send.at[d]).wait()


def solution(mesh):
    def step(x, w_gate, w_up, w_down):
        rows, dim = x.shape
        ff = w_gate.shape[1]
        r, nt = rows // 2, dim // NU
        n = mesh.shape["tp"]
        npc = 2 * (dim // KC) + 2
        vm, dma = pltpu.VMEM, pltpu.SemaphoreType.DMA
        return pl.pallas_call(
            _kernel,
            out_shape=pltpu.VMEM((rows, dim), BF16),
            in_specs=[pl.BlockSpec(memory_space=pl.ANY)] * 4,
            out_specs=pl.BlockSpec(memory_space=pltpu.VMEM),
            scratch_shapes=[
                vm((2, n * r, dim), BF16),
                vm((n * r, ff), F32),
                vm((n * r, ff), F32),
                vm((n * r, ff), BF16),
                vm((RING, KC, NU), BF16),
                vm((nt, r, NU), F32),
                vm((nt, r, NU), F32),
                vm((2 * nt, r, NU), BF16),
                vm((2 * nt, r, NU), BF16),
                vm((2 * nt, r, NU), BF16),
                vm((nt, r, NU), BF16),
                vm((nt, r, NU), BF16),
                vm((nt, r, NU), BF16),
                dma((2,)),
                dma((2,)),
                dma((2,)),
                dma((2,)),
                dma((2, npc)),
                dma((2, npc)),
                dma((3,)),
                dma((2 * nt,)),
                dma((2 * nt,)),
                dma((2 * nt,)),
            ],
            compiler_params=pltpu.CompilerParams(
                collective_id=0, has_side_effects=True, vmem_limit_bytes=67043328 - 2 * rows * dim),
        )(x, w_gate, w_up, w_down)

    return jax.shard_map(
        step, mesh=mesh,
        in_specs=(P(("dp", "tp"), None), P(None, "tp"), P(None, "tp"), P("tp", None)),
        out_specs=P(("dp", "tp"), None), check_vma=False)
```

time: 190 us -> 188 us (0.989)
  Pallas kernels: 188 us -> 186 us
    pallas_call x1, Pallas kernels: 188 us -> 186 us  [step(): pl.pallas_call(_kernel, out_shape=pltpu.VMEM((rows, dim), BF16), in_specs...]
where the time goes in v3:
time: 188 us
  Pallas kernels  186 us (99%)
    pallas_call x1, Pallas kernels, step(): pl.pallas_call(_kernel, out_shape=pltpu.VMEM((rows, dim), BF16), in_specs...  186 us

profile of v3, /device:TPU:112, one launch (start us, length us, event | category | flops | bytes accessed | tf_op | source)
XLA Modules:
  0.0 187.5 jit_solution(11851877762633271034)
XLA Ops:
  0.0 186.1 %shard_map.46 = bf16[160,7168]{1,0:T(8,128)(2,1)S(1)} custom-call(bf16[160,7168]{1,0:T(8,128)(2,1)} %x_ref.1, bf16[7168,5120]{1,0:T(8,128)(2,1)} %wg_ref.1, bf16[7168,5120]{1,0:T(8,128)(2,1)} %wu_ref.1, bf16[5120,7168]{1,0:T(8,128)(2,1)} %wd_ref.1), custom_call_target="tpu_custom_call" | custom-call | tf_op jit(solution)/shard_map/pallas_call | solution.py:329
  186.1 1.4 copy.6
